TPU v7x, 32 devices: a whole 2x2x4 slice. The times are simulated.
32 devices in a mesh: section: 2 (over core), vocab: 16 (over z, y, x).
Axes of the slice: x: 2, y: 2, z: 4, core: 2. Of those that a mesh axis runs over, the one named last changes fastest.
Arguments:
- hidden_in: bfloat16 [2, 256, 7168], P(None, ('section', 'vocab')), may hold values from -6 to 6
- gain_ffn: float32 [7168], replicated, may hold values from 0.4 to 1.6
- w_gate: bfloat16 [7168, 18432], P(None, ('section', 'vocab')), may hold values from -0.0625 to 0.0625
- w_up: bfloat16 [7168, 18432], P(None, ('section', 'vocab')), may hold values from -0.0625 to 0.0625
- w_down: bfloat16 [18432, 7168], P(('section', 'vocab')), may hold values from -0.046875 to 0.046875
- gain_final: float32 [7168], replicated, may hold values from 0.4 to 1.6
- head_weight: bfloat16 [7168, 129280], P(None, ('section', 'vocab')), may hold values from -4.5 to 4.5
- sampled_ids: int32 [2, 256], replicated, may hold values from 0 to 129279
- seq_ids: int32 [2, 256], P(None, ('section', 'vocab')), may hold values from 0 to 7, never falling along the last dimension, each value on 1 to 128 neighbouring positions
Outputs:
- token_logprob: float32 [2, 256], P(None, ('section', 'vocab'))
- log_norm: float32 [2, 256], P(None, ('section', 'vocab'))
- top_mass: float32 [2, 256], P(None, ('section', 'vocab'))
- seq_logprob: float32 [2, 8], replicated
All inputs are finite; a program needn't handle non-finite values.
Results may differ from a plain program's by a relative error of at most 0.006.
Values may be sent and summed in bfloat16 or wider, within the bound.
No kernel may reach another device: no remote copies, remote signals or barrier semaphores. Data moves between devices by JAX's collectives and lax.ppermute only.
A program may use at most 192 MiB of HBM per device.

v0:
```python
import jax
import jax.numpy as jnp
from jax import lax
from jax.sharding import PartitionSpec as P

SEQS = 8
TOPK = 20
epsilon = 1e-06


def rms_norm(values, scale_gain):
    wide = values.astype(jnp.float32)
    square_mean = jnp.mean(wide * wide, axis=-1, keepdims=True)
    return (wide * lax.rsqrt(square_mean + epsilon) * scale_gain).astype(jnp.bfloat16)


def largest(values):
    return lax.sort(values, dimension=values.ndim - 1)[..., -TOPK:]


def finish(peak_value, sum_total, sampled_logit, leaders_all):
    log_norm = peak_value + jnp.log(sum_total)
    top_mass = jnp.sum(jnp.exp(leaders_all - log_norm[:, None]), axis=1)
    return (sampled_logit - log_norm, log_norm, top_mass)


def combine_sources(pieces):
    maxima, exp_sums, sampled_parts, top_values = pieces
    peak_value = jnp.max(maxima, axis=0)
    sum_total = jnp.sum(exp_sums * jnp.exp(maxima - peak_value[None, :]), axis=0)
    sampled_logit = jnp.sum(sampled_parts, axis=0)
    item_count = top_values.shape[1]
    pooled = jnp.transpose(top_values, (1, 0, 2)).reshape(item_count, -1)
    leaders_all = largest(pooled)
    return finish(peak_value, sum_total, sampled_logit, leaders_all)


def body(hidden_in, gain_ffn, w_gate, w_up, w_down, gain_final, head_weight, sampled_ids, seq_ids):
    row_count = hidden_in.shape[1]
    shard_width = head_weight.shape[1]
    position = lax.axis_index(("section", "vocab"))
    group_count = lax.axis_size(("section", "vocab"))
    columns = lax.broadcasted_iota(jnp.int32, (1, shard_width), 1) + position * shard_width
    logprob_list = []
    norm_list = []
    mass_list = []
    partials = []
    for microbatch in range(hidden_in.shape[0]):
        own_rows = hidden_in[microbatch]
        gathered = lax.all_gather(own_rows, ("section", "vocab"), axis=0, tiled=True)
        normed = rms_norm(gathered, gain_ffn)
        gate_proj = jnp.dot(normed, w_gate, preferred_element_type=jnp.float32)
        up_proj = jnp.dot(normed, w_up, preferred_element_type=jnp.float32)
        hidden_act = (jax.nn.silu(gate_proj) * up_proj).astype(jnp.bfloat16)
        branch = lax.psum(
            jnp.dot(hidden_act, w_down, preferred_element_type=jnp.float32), ("section", "vocab")
        )
        residual = (gathered.astype(jnp.float32) + branch).astype(jnp.bfloat16)
        scaled = rms_norm(residual, gain_final)
        logits = jnp.dot(scaled, head_weight, preferred_element_type=jnp.float32)
        token_ids = sampled_ids[microbatch]
        matches = columns == token_ids[:, None]
        sampled_part = jnp.sum(jnp.where(matches, logits, 0.0), axis=1)
        leaders = largest(logits)
        local_peak = jnp.max(logits, axis=1).reshape(group_count, row_count)
        local_total = jnp.sum(jnp.exp(logits - jnp.max(logits, axis=1)[:, None]), axis=1).reshape(
            group_count, row_count
        )
        sampled_block = sampled_part.reshape(group_count, row_count)
        leader_block = leaders.reshape(group_count, row_count, TOPK)
        token_logprob, log_norm, top_mass = combine_sources(
            (
                lax.all_to_all(
                    local_peak, ("section", "vocab"), split_axis=0, concat_axis=0, tiled=True
                ),
                lax.all_to_all(
                    local_total, ("section", "vocab"), split_axis=0, concat_axis=0, tiled=True
                ),
                lax.all_to_all(
                    sampled_block, ("section", "vocab"), split_axis=0, concat_axis=0, tiled=True
                ),
                lax.all_to_all(
                    leader_block, ("section", "vocab"), split_axis=0, concat_axis=0, tiled=True
                ),
            )
        )
        onehot = (
            seq_ids[microbatch][:, None] == jnp.arange(SEQS, dtype=jnp.int32)[None, :]
        ).astype(jnp.float32)
        partials.append(jnp.sum(token_logprob[:, None] * onehot, axis=0))
        logprob_list.append(token_logprob)
        norm_list.append(log_norm)
        mass_list.append(top_mass)
    seq_logprob = lax.psum(jnp.stack(partials), ("section", "vocab"))
    return (jnp.stack(logprob_list), jnp.stack(norm_list), jnp.stack(mass_list), seq_logprob)


def solution(mesh):
    in_specs = (
        P(None, ("section", "vocab"), None),
        P(),
        P(None, ("section", "vocab")),
        P(None, ("section", "vocab")),
        P(("section", "vocab"), None),
        P(),
        P(None, ("section", "vocab")),
        P(),
        P(None, ("section", "vocab")),
    )
    out_specs = (
        P(None, ("section", "vocab")),
        P(None, ("section", "vocab")),
        P(None, ("section", "vocab")),
        P(),
    )
    return jax.shard_map(body, mesh=mesh, in_specs=in_specs, out_specs=out_specs, check_vma=False)
```

profile of v0, /device:TPU:0, one launch (start us, length us, event | category | flops | bytes accessed | tf_op | source)
XLA Modules:
  0.0 1247.0 jit_solution(10427038897527076204)
XLA Ops:
  9.7 64.3 %all-gather.5.cloned.1.call-done = bf16[1,256,7168]{2,1,0:T(8,128)(2,1)} async-done(((bf16[1,8,7168]{2,1,0:T(8,128)(2,1)}), bf16[1,256,7168]{2,1,0:T(8,128)(2,1)}) %all-gather.5.cloned.1.call-update) | async-done | bytes 3670032 | tf_op jit(solution)/shard_map/all_gather | solution.py:50
  76.9 59.1 %all-gather.7.cloned.1.call-done = bf16[1,256,7168]{2,1,0:T(8,128)(2,1)} async-done(((bf16[1,8,7168]{2,1,0:T(8,128)(2,1)}), bf16[1,256,7168]{2,1,0:T(8,128)(2,1)}) %all-gather.7.cloned.1.call-update) | async-done | bytes 3670032 | tf_op jit(solution)/shard_map/all_gather | solution.py:50
  139.0 7.0 fusion.28
  148.5 19.7 %fusion.34 = f32[256,7168]{1,0:T(8,128)} fusion(bf16[576,7168]{1,0:T(8,128)(2,1)} %param.13, bf16[7168,576]{0,1:T(8,128)(2,1)} %param.12, bf16[1,256,7168]{2,1,0:T(8,128)(2,1)} %all-gather.5.cloned.1.call-done, f32[7168]{0:T(1024)S(1)} %copy-done.3, f32[256]{0:T(256)S(1)} %add_rsqrt_fusion.3, f32[256,576]{0,1:T(8,128)S(1)} %fusion.28), kind=kOutput, calls=%fused_computation.41 | convolution fusion | flops 4236083200 | bytes 28144640 | tf_op jit(solution)/shard_map/dot_general | solution.py:56
  168.2 19.3 %fusion.31 = f32[256,7168]{1,0:T(8,128)} fusion(bf16[576,7168]{1,0:T(8,128)(2,1)} %param.13, bf16[7168,576]{0,1:T(8,128)(2,1)} %param.12, bf16[1,256,7168]{2,1,0:T(8,128)(2,1)} %all-gather.7.cloned.1.call-done, f32[256]{0:T(256)S(1)} %add_rsqrt_fusion.1, f32[7168]{0:T(1024)S(1)} %copy-done.3, f32[256,576]{0,1:T(8,128)S(1)} %fusion.25), kind=kOutput, calls=%fused_computation.40 | convolution fusion | flops 4236083200 | bytes 28144640 | tf_op jit(solution)/shard_map/dot_general | solution.py:56
  188.2 251.1 %all-reduce.3.cloned.1.call-done = (f32[256,7168]{1,0:T(8,128)}, f32[256,7168]{1,0:T(8,128)}) async-done(((f32[256,7168]{1,0:T(8,128)}, f32[256,7168]{1,0:T(8,128)}), (f32[256,7168]{1,0:T(8,128)}, f32[256,7168]{1,0:T(8,128)})) %all-reduce.3.cloned.1.call-update) | async-done | bytes 14680080 | tf_op jit(solution)/shard_map/psum | solution.py:55
  439.3 8.4 fusion
  447.7 28.2 %fusion.46 = (f32[256]{0:T(256)S(1)}, f32[256,4040]{0,1:T(8,128)}) fusion(bf16[7168,4040]{0,1:T(8,128)(2,1)} %param.15, f32[7168]{0:T(1024)S(1)} %copy-done.4, f32[256]{0:T(256)S(1)} %add_rsqrt_fusion.2, f32[256,7168]{1,0:T(8,128)} %get-tuple-element.25, bf16[1,256,7168]{2,1,0:T(8,128)(2,1)} %all-gather.5.cloned.1.call-done), kind=kOutput, calls=%fused_computation.75 | convolution fusion | flops 14840743936 | bytes 73095168 | tf_op jit(solution)/shard_map/dot_general | solution.py:60
  476.6 4.8 all-to-all-start.1
  483.6 296.8 %sort.56 = (f32[256,4040]{0,1:T(8,128)}, s32[256,4040]{0,1:T(8,128)}) sort(f32[256,4040]{0,1:T(8,128)} %get-tuple-element.39, s32[256,4040]{0,1:T(8,128)} %iota.24.clone), dimensions={1}, to_apply=%region_18.19 | sort | flops 20684800 | bytes 16547840 | tf_op jit(solution)/shard_map/sort | solution.py:18
  780.4 5.6 copy.39
  786.0 28.4 %fusion.47 = (f32[256]{0:T(256)S(1)}, f32[256,4040]{0,1:T(8,128)}) fusion(bf16[7168,4040]{0,1:T(8,128)(2,1)} %param.15, f32[256]{0:T(256)S(1)} %add_rsqrt_fusion, f32[7168]{0:T(1024)S(1)} %copy-done.4, f32[256,7168]{1,0:T(8,128)} %get-tuple-element.24, bf16[1,256,7168]{2,1,0:T(8,128)(2,1)} %all-gather.7.cloned.1.call-done), kind=kOutput, calls=%fused_computation.76 | convolution fusion | flops 14840743936 | bytes 73095168 | tf_op jit(solution)/shard_map/dot_general | solution.py:60
  814.3 5.1 exponential_reduce_fusion.1
  820.4 296.9 %sort.58 = (f32[256,4040]{0,1:T(8,128)}, s32[256,4040]{0,1:T(8,128)}) sort(f32[256,4040]{0,1:T(8,128)} %get-tuple-element.41, s32[256,4040]{0,1:T(8,128)} %iota.24.clone), dimensions={1}, to_apply=%region_21.22 | sort | flops 20684800 | bytes 16547840 | tf_op jit(solution)/shard_map/sort | solution.py:18
  1117.9 5.5 copy.43
  1123.5 5.9 all-to-all-start.2
  1140.6 7.1 all-to-all-done
  1150.3 7.1 all-to-all-done.4
  1160.0 7.1 all-to-all-done.5
  1169.6 7.1 all-to-all-done.3
  1180.6 40.4 %psum.23 = f32[2,8]{1,0:T(2,128)} all-reduce(f32[2,8]{1,0:T(2,128)S(1)} %pad_maximum_fusion.3), channel_id=1, replica_groups=mesh['section'=2,'vocab'=16] {'section','vocab'}, use_global_device_ids=true, to_apply=%region_26.27 | all-reduce | flops 16 | bytes 128 | tf_op jit(solution)/shard_map/psum | solution.py:94
  1221.0 5.0 all-to-all-start.7
  1227.6 4.9 sort.57
  1234.3 4.9 sort.59
  (81 shorter events, 42.8 us)
Async XLA Ops:
  7.2 131.8 %copy-start.3 = (f32[7168]{0:T(1024)S(1)}, f32[7168]{0:T(1024)}, u32[]{:S(2)}) copy-start(f32[7168]{0:T(1024)} %param.10) | copy-start | bytes 86020
  7.2 66.8 %all-gather.5.cloned.1.call-start = ((), (), s32[]{:S(2)}) async-start(), calls=%async_computation.8 | async-start | bytes 3784704 | tf_op jit(solution)/shard_map/all_gather | solution.py:50
  8.9 127.0 %all-gather.7.cloned.1.call-start = ((), (), s32[]{:S(2)}) async-start(), calls=%async_computation.9 | async-start | bytes 3784704 | tf_op jit(solution)/shard_map/all_gather | solution.py:50
  9.6 429.6 %all-reduce.3.cloned.1.call-start = ((), (), s32[]{:S(2)}) async-start(), calls=%async_computation.10 | async-start | bytes 29360128 | tf_op jit(solution)/shard_map/psum | solution.py:55
  135.9 10.1 slice-start
  138.9 7.1 copy-start
  139.0 7.1 slice-start.1
  187.5 0.7 copy-start.2
  187.5 0.7 copy-start.1
  439.3 8.4 copy-start.4
  476.6 646.9 %all-to-all-start.1 = ((f32[32,1,8]{2,1,0:T(1,128)}), f32[32,1,8]{2,1,0:T(1,128)S(1)}, u32[]{:S(2)}, u32[]{:S(2)}) async-start(f32[32,1,8]{2,1,0:T(1,128)} %bitcast.5), calls=%async_computation.1 | async-start | bytes 32768 | tf_op jit(solution)/shard_map/all_to_all | solution.py:73
  1123.5 13.1 %all-to-all-start.2 = ((f32[32,1,8]{2,1,0:T(1,128)}), f32[32,1,8]{2,1,0:T(1,128)S(1)}, u32[]{:S(2)}, u32[]{:S(2)}) async-start(f32[32,1,8]{2,1,0:T(1,128)} %bitcast.6), calls=%async_computation.2 | async-start | bytes 32768 | tf_op jit(solution)/shard_map/all_to_all | solution.py:76
  1136.6 11.2 all-to-all-start
  1147.8 9.7 all-to-all-start.4
  1157.4 9.6 all-to-all-start.5
  1167.1 9.6 all-to-all-start.3
  1176.7 44.3 %all-to-all-start.6 = ((f32[32,1,160]{2,1,0:T(1,128)}), f32[32,1,160]{2,1,0:T(1,128)S(1)}, u32[]{:S(2)}, u32[]{:S(2)}) async-start(f32[32,1,160]{2,1,0:T(1,128)} %reshape.189), calls=%async_computation.6 | async-start | bytes 65536 | tf_op jit(solution)/shard_map/all_to_all | solution.py:82
  1221.0 12.2 all-to-all-start.7
Sparse Core Ops, SparseCore 0:
  10.8 63.1 all-gather.4
  76.9 59.0 all-gather.6
  187.7 251.5 all-reduce.2
where the time goes:
time: 1260 us; the launch traced here: 1250 us
  other arithmetic  627 us (50%)
  waiting for transfers between devices  406 us (32%)
  matrix products  105 us (8%)
  blocking collectives  40.4 us (3%)
  starting transfers between devices  29.9 us (2%)
  local copies, waits for them, and re-layouts  24.3 us (2%)
  between operations  14.5 us (1%)
    sort x4, other arithmetic, largest(): return lax.sort(values, dimension=values.ndim - 1)[..., -TOPK:]  604 us
    psum x1, waiting for transfers between devices, body(): lax.psum(jnp.dot(hidden_act, w_down, preferred_element_type=jnp.float32),...  251 us
    all_gather x2, waiting for transfers between devices, body(): lax.all_gather(own_rows, ('section', 'vocab'), axis=0, tiled=True)  123 us
    dot_general x2, matrix products, body(): logits = jnp.dot(scaled, head_weight, preferred_element_type=jnp.float32)  56.6 us
    psum x1, blocking collectives, body(): seq_logprob = lax.psum(jnp.stack(partials), ('section', 'vocab'))  40.4 us
    dot_general x2, matrix products, body(): jnp.dot(hidden_act, w_down, preferred_element_type=jnp.float32)  39 us
  transfers between devices with their start and end apart: 11, of which 9 were waited for; matrix products, arithmetic and copies ran while one was open for 53% of the time, Pallas kernels for 0%

commit v1 on v0

--- a/solution.py
+++ b/solution.py
@@ -53,7 +53,8 @@
         up_proj = jnp.dot(normed, w_up, preferred_element_type=jnp.float32)
         hidden_act = (jax.nn.silu(gate_proj) * up_proj).astype(jnp.bfloat16)
         branch = lax.psum(
-            jnp.dot(hidden_act, w_down, preferred_element_type=jnp.float32), ("section", "vocab")
+            lax.psum(jnp.dot(hidden_act, w_down, preferred_element_type=jnp.float32), "vocab"),
+            "section",
         )
         residual = (gathered.astype(jnp.float32) + branch).astype(jnp.bfloat16)
         scaled = rms_norm(residual, gain_final)

time: 1260 us -> 1470 us (1.17)
  waiting for transfers between devices: 406 us -> 614 us
    psum x1, waiting for transfers between devices: 251 us -> 405 us  [body(): lax.psum(jnp.dot(hidden_act, w_down, preferred_element_type=jnp.float32),...]
    psum x0 -> x1, waiting for transfers between devices: none -> 54.3 us  [body(): lax.psum(lax.psum(jnp.dot(hidden_act, w_down, preferred_element_type=jnp....]
  transfers between devices with their start and end apart: 11 -> 12, of which waited for: 9 -> 10; matrix products, arithmetic and copies ran while one was open for 53% -> 24% of each run, Pallas kernels for 0% -> 0%
where the time goes in v1:
time: 1470 us; the launch traced here: 1460 us
  other arithmetic  627 us (43%)
  waiting for transfers between devices  614 us (42%)
  matrix products  105 us (7%)
  blocking collectives  40.4 us (3%)
  starting transfers between devices  31.2 us (2%)
  local copies, waits for them, and re-layouts  24.3 us (2%)
    sort x4, other arithmetic, largest(): return lax.sort(values, dimension=values.ndim - 1)[..., -TOPK:]  604 us
    psum x1, waiting for transfers between devices, body(): lax.psum(jnp.dot(hidden_act, w_down, preferred_element_type=jnp.float32),...  405 us
    all_gather x2, waiting for transfers between devices, body(): lax.all_gather(own_rows, ('section', 'vocab'), axis=0, tiled=True)  123 us
    dot_general x2, matrix products, body(): logits = jnp.dot(scaled, head_weight, preferred_element_type=jnp.float32)  56.4 us
    psum x1, waiting for transfers between devices, body(): lax.psum(lax.psum(jnp.dot(hidden_act, w_down, preferred_element_type=jnp....  54.3 us
    psum x1, blocking collectives, body(): seq_logprob = lax.psum(jnp.stack(partials), ('section', 'vocab'))  40.4 us
    dot_general x2, matrix products, body(): jnp.dot(hidden_act, w_down, preferred_element_type=jnp.float32)  38.9 us
  transfers between devices with their start and end apart: 12, of which 10 were waited for; matrix products, arithmetic and copies ran while one was open for 24% of the time, Pallas kernels for 0%

profile of v1, /device:TPU:0, one launch (start us, length us, event | category | flops | bytes accessed | tf_op | source)
XLA Modules:
  0.0 1456.1 jit_solution(13081088662104461363)
XLA Ops:
  9.7 64.3 %all-gather.5.cloned.1.call-done = bf16[1,256,7168]{2,1,0:T(8,128)(2,1)} async-done(((bf16[1,8,7168]{2,1,0:T(8,128)(2,1)}), bf16[1,256,7168]{2,1,0:T(8,128)(2,1)}) %all-gather.5.cloned.1.call-update) | async-done | bytes 3670032 | tf_op jit(solution)/shard_map/all_gather | solution.py:50
  76.9 59.1 %all-gather.7.cloned.1.call-done = bf16[1,256,7168]{2,1,0:T(8,128)(2,1)} async-done(((bf16[1,8,7168]{2,1,0:T(8,128)(2,1)}), bf16[1,256,7168]{2,1,0:T(8,128)(2,1)}) %all-gather.7.cloned.1.call-update) | async-done | bytes 3670032 | tf_op jit(solution)/shard_map/all_gather | solution.py:50
  139.0 7.0 fusion.28
  148.5 19.6 %fusion.34 = f32[256,7168]{1,0:T(8,128)} fusion(bf16[576,7168]{1,0:T(8,128)(2,1)} %param.13, bf16[7168,576]{0,1:T(8,128)(2,1)} %param.12, bf16[1,256,7168]{2,1,0:T(8,128)(2,1)} %all-gather.5.cloned.1.call-done, f32[7168]{0:T(1024)S(1)} %copy-done.3, f32[256]{0:T(256)S(1)} %add_rsqrt_fusion.3, f32[256,576]{0,1:T(8,128)S(1)} %fusion.28), kind=kOutput, calls=%fused_computation.41 | convolution fusion | flops 4236083200 | bytes 28144640 | tf_op jit(solution)/shard_map/dot_general | solution.py:56
  168.0 19.4 %fusion.31 = f32[256,7168]{1,0:T(8,128)} fusion(bf16[576,7168]{1,0:T(8,128)(2,1)} %param.13, bf16[7168,576]{0,1:T(8,128)(2,1)} %param.12, bf16[1,256,7168]{2,1,0:T(8,128)(2,1)} %all-gather.7.cloned.1.call-done, f32[256]{0:T(256)S(1)} %add_rsqrt_fusion.1, f32[7168]{0:T(1024)S(1)} %copy-done.3, f32[256,576]{0,1:T(8,128)S(1)} %fusion.25), kind=kOutput, calls=%fused_computation.40 | convolution fusion | flops 4236083200 | bytes 28144640 | tf_op jit(solution)/shard_map/dot_general | solution.py:56
  187.9 404.8 %all-reduce.5.cloned.1.call-done = (f32[256,7168]{1,0:T(8,128)}, f32[256,7168]{1,0:T(8,128)}) async-done(((f32[256,7168]{1,0:T(8,128)}, f32[256,7168]{1,0:T(8,128)}), (f32[256,7168]{1,0:T(8,128)}, f32[256,7168]{1,0:T(8,128)})) %all-reduce.5.cloned.1.call-update) | async-done | bytes 14680080 | tf_op jit(solution)/shard_map/psum | solution.py:56
  593.5 54.3 %all-reduce.7.cloned.1.call-done = (f32[256,7168]{1,0:T(8,128)}, f32[256,7168]{1,0:T(8,128)}) async-done(((f32[256,7168]{1,0:T(8,128)}, f32[256,7168]{1,0:T(8,128)}), (f32[256,7168]{1,0:T(8,128)}, f32[256,7168]{1,0:T(8,128)})) %all-reduce.7.cloned.1.call-update) | async-done | bytes 14680080 | tf_op jit(solution)/shard_map/psum | solution.py:55
  647.8 8.4 fusion
  656.2 28.2 %fusion.46 = (f32[256]{0:T(256)S(1)}, f32[256,4040]{0,1:T(8,128)}) fusion(bf16[7168,4040]{0,1:T(8,128)(2,1)} %param.15, f32[7168]{0:T(1024)S(1)} %copy-done.4, f32[256]{0:T(256)S(1)} %add_rsqrt_fusion.2, f32[256,7168]{1,0:T(8,128)} %get-tuple-element.27, bf16[1,256,7168]{2,1,0:T(8,128)(2,1)} %all-gather.5.cloned.1.call-done), kind=kOutput, calls=%fused_computation.75 | convolution fusion | flops 14840743936 | bytes 73095168 | tf_op jit(solution)/shard_map/dot_general | solution.py:61
  686.6 296.8 %sort.56 = (f32[256,4040]{0,1:T(8,128)}, s32[256,4040]{0,1:T(8,128)}) sort(f32[256,4040]{0,1:T(8,128)} %get-tuple-element.41, s32[256,4040]{0,1:T(8,128)} %iota.24.clone), dimensions={1}, to_apply=%region_20.21 | sort | flops 20684800 | bytes 16547840 | tf_op jit(solution)/shard_map/sort | solution.py:18
  983.5 5.6 copy.39
  989.7 5.8 all-to-all-start.1
  995.5 28.2 %fusion.47 = (f32[256]{0:T(256)S(1)}, f32[256,4040]{0,1:T(8,128)}) fusion(bf16[7168,4040]{0,1:T(8,128)(2,1)} %param.15, f32[256]{0:T(256)S(1)} %add_rsqrt_fusion, f32[7168]{0:T(1024)S(1)} %copy-done.4, f32[256,7168]{1,0:T(8,128)} %get-tuple-element.26, bf16[1,256,7168]{2,1,0:T(8,128)(2,1)} %all-gather.7.cloned.1.call-done), kind=kOutput, calls=%fused_computation.76 | convolution fusion | flops 14840743936 | bytes 73095168 | tf_op jit(solution)/shard_map/dot_general | solution.py:61
  1023.7 5.1 exponential_reduce_fusion.1
  1029.8 296.8 %sort.58 = (f32[256,4040]{0,1:T(8,128)}, s32[256,4040]{0,1:T(8,128)}) sort(f32[256,4040]{0,1:T(8,128)} %get-tuple-element.43, s32[256,4040]{0,1:T(8,128)} %iota.24.clone), dimensions={1}, to_apply=%region_23.24 | sort | flops 20684800 | bytes 16547840 | tf_op jit(solution)/shard_map/sort | solution.py:18
  1327.3 5.5 copy.43
  1332.8 5.8 all-to-all-start.2
  1349.9 7.1 all-to-all-done
  1359.6 7.1 all-to-all-done.4
  1369.2 7.1 all-to-all-done.5
  1378.8 7.1 all-to-all-done.3
  1389.9 40.4 %psum.39 = f32[2,8]{1,0:T(2,128)} all-reduce(f32[2,8]{1,0:T(2,128)S(1)} %pad_maximum_fusion.3), channel_id=1, replica_groups=mesh['section'=2,'vocab'=16] {'section','vocab'}, use_global_device_ids=true, to_apply=%region_28.29 | all-reduce | flops 16 | bytes 128 | tf_op jit(solution)/shard_map/psum | solution.py:95
  1430.3 5.0 all-to-all-start.7
  1436.8 4.9 sort.57
  (84 shorter events, 48.3 us)
Async XLA Ops:
  7.2 131.8 %copy-start.3 = (f32[7168]{0:T(1024)S(1)}, f32[7168]{0:T(1024)}, u32[]{:S(2)}) copy-start(f32[7168]{0:T(1024)} %param.10) | copy-start | bytes 86020
  7.2 66.8 %all-gather.5.cloned.1.call-start = ((), (), s32[]{:S(2)}) async-start(), calls=%async_computation.8 | async-start | bytes 3784704 | tf_op jit(solution)/shard_map/all_gather | solution.py:50
  8.9 127.0 %all-gather.7.cloned.1.call-start = ((), (), s32[]{:S(2)}) async-start(), calls=%async_computation.9 | async-start | bytes 3784704 | tf_op jit(solution)/shard_map/all_gather | solution.py:50
  9.6 583.1 %all-reduce.5.cloned.1.call-start = ((), (), s32[]{:S(2)}) async-start(), calls=%async_computation.10 | async-start | bytes 29360128 | tf_op jit(solution)/shard_map/psum | solution.py:56
  135.9 10.1 slice-start
  138.9 7.1 copy-start
  139.0 7.1 slice-start.1
  187.4 460.3 %all-reduce.7.cloned.1.call-start = ((), (), s32[]{:S(2)}) async-start(), calls=%async_computation.11 | async-start | bytes 29360128 | tf_op jit(solution)/shard_map/psum | solution.py:55
  592.8 0.7 copy-start.2
  592.8 0.7 copy-start.1
  647.8 8.4 copy-start.4
  989.7 343.1 %all-to-all-start.1 = ((f32[32,1,8]{2,1,0:T(1,128)}), f32[32,1,8]{2,1,0:T(1,128)S(1)}, u32[]{:S(2)}, u32[]{:S(2)}) async-start(f32[32,1,8]{2,1,0:T(1,128)} %bitcast.5), calls=%async_computation.1 | async-start | bytes 32768 | tf_op jit(solution)/shard_map/all_to_all | solution.py:74
  1332.8 13.0 all-to-all-start.2
  1345.8 11.2 all-to-all-start
  1357.0 9.7 all-to-all-start.4
  1366.7 9.6 all-to-all-start.5
  1376.3 9.6 all-to-all-start.3
  1385.9 44.3 %all-to-all-start.6 = ((f32[32,1,160]{2,1,0:T(1,128)}), f32[32,1,160]{2,1,0:T(1,128)S(1)}, u32[]{:S(2)}, u32[]{:S(2)}) async-start(f32[32,1,160]{2,1,0:T(1,128)} %reshape.189), calls=%async_computation.6 | async-start | bytes 65536 | tf_op jit(solution)/shard_map/all_to_all | solution.py:83
  1430.3 12.2 all-to-all-start.7
Sparse Core Ops, SparseCore 0:
  10.8 63.1 all-gather.4
  76.9 59.0 all-gather.6
  187.5 405.1 all-reduce.4
  595.2 52.5 all-reduce.6
